TPU v7x, 32 devices: a whole 2x2x4 slice. The times are simulated.
32 devices in a mesh: shot: 2 (over x), gz: 16 (over z, y, core).
Axes of the slice: x: 2, y: 2, z: 4, core: 2. Of those that a mesh axis runs over, the one named last changes fastest.
Arguments:
- source_now: float32 [256, 128, 128], P(('shot', 'gz')), parts along dimension 0, may hold values from -6 to 6
- source_before: float32 [256, 128, 128], P(('shot', 'gz')), parts along dimension 0, may hold values from -6 to 6
- receiver_now: float32 [256, 128, 128], P(('shot', 'gz')), parts along dimension 0, may hold values from -6 to 6
- receiver_before: float32 [256, 128, 128], P(('shot', 'gz')), parts along dimension 0, may hold values from -6 to 6
- speed_term: float32 [128, 128, 128], P('gz'), may hold values from 0.03 to 0.18
- saved_faces: float32 [24, 8, 128, 128], P('shot', None, 'gz'), parts along dimension 0, may hold values from -6 to 6
- face_steps: int32 [12], replicated, may hold values from 0 to 11, each once
- traces: bfloat16 [24, 128, 128], P('shot'), parts along dimension 0, may hold values from -6 to 6
- lag_offsets: int32 [8], replicated, may hold values from -8 to 8, as said below
- snap_phase: int32 [2], replicated, may hold values from 0 to 5
Outputs:
- image_out: bfloat16 [16, 128, 128, 128], P('shot', None, 'gz'), parts along dimension 0
- source_final: float32 [256, 128, 128], P(('shot', 'gz')), parts along dimension 0
- receiver_final: float32 [256, 128, 128], P(('shot', 'gz')), parts along dimension 0
There are 2 independent parts, one for each index of `shot`. A program takes and returns all parts, laid end to end along the dimension named above; an argument that names none is the same for every part. Nothing has to cross between parts.
Inputs may be any that keep to these rules, and one draw needn't show every extreme that they name: `face_steps`: each of the 12 saved slots belongs to exactly one step. `lag_offsets`: the 8 offsets are different, and both ends of the range occur.
All inputs are finite; a program needn't handle non-finite values.
Results may differ from a plain program's by a relative error of at most 0.001.
Values sent between devices are 32-bit elements; how exact they have to be, the bound alone decides.
A program may use at most 64 MiB of HBM per device.

v0:
```python
import functools

import jax
import jax.numpy as jnp
import numpy as np
from jax import lax
from jax.experimental import pallas as pl
from jax.experimental.pallas import tpu as pltpu
from jax.sharding import PartitionSpec as P

SNAP_EVERY = 6
SNAPS = 2
STEPS = SNAPS * SNAP_EVERY
HALO = 4
ROWS = 8
CHUNK = 4

stencil_weights = (-205.0 / 72.0, 8.0 / 5.0, -1.0 / 5.0, 8.0 / 315.0, -1.0 / 560.0)
damping = 0.25
smoothing = 16.0
MESH = pl.DeviceIdType.MESH


def lateral_weights(breadth):
    apart = np.abs(np.arange(breadth)[:, None] - np.arange(breadth)[None, :])
    band = np.zeros((breadth, breadth), np.float64)
    band[apart == 0] = 3.0 * stencil_weights[0]
    for offset in range(1, 5):
        band[apart == offset] = stencil_weights[offset]
    band = jnp.asarray(band, jnp.float32)
    high = band.astype(jnp.bfloat16)
    low = (band - high.astype(jnp.float32)).astype(jnp.bfloat16)
    return jnp.concatenate([high, high], axis=0), low


def wave_kernel(
    count,
    group,
    strip,
    phase_ref,
    src_now,
    src_old,
    rec_now,
    rec_old,
    speed,
    faces,
    traces,
    weights_a,
    weights_b,
    strips_out,
    src_out,
    rec_out,
    field,
    factor,
    edges,
    snaps,
    load_send,
    load_recv,
    load_own,
    halo_send,
    halo_recv,
    strip_send,
    strip_recv,
    strip_own,
    back_send,
    back_recv,
    back_own,
):
    me = lax.axis_index("gz")
    outer = count // group
    a = me // group
    b = me % group
    q = (group - b) % group
    thin = src_now.shape[0]
    layers = thin * group
    height = src_now.shape[1] // group
    breadth = src_now.shape[2]
    inner = pl.ds(ROWS, height)

    def landing(index, sender):
        planes = pl.ds(HALO + sender * thin, thin)
        flat = pl.ds(sender * thin, thin)
        if index == 0:
            return factor.at[flat]
        if index == 5:
            return edges.at[flat]
        return {
            1: field.at[1, 0, planes, inner],
            2: field.at[1, 1, planes, inner],
            3: field.at[0, 0, planes, inner],
            4: field.at[0, 1, planes, inner],
        }[index]

    inputs = (speed, rec_now, rec_old, src_now, src_old, faces)

    def rows_of(quarter):
        return pl.ds(pl.multiple_of(quarter * height, ROWS), height)

    def load_copy(index, shift, sender, target):
        return pltpu.make_async_remote_copy(
            src_ref=inputs[index].at[:, rows_of((group - target) % group), :],
            dst_ref=landing(index, sender),
            send_sem=load_send.at[index, shift],
            recv_sem=load_recv.at[index, shift],
            device_id={"gz": a * group + target},
            device_id_type=MESH,
        )

    def own_copy(index):
        return pltpu.make_async_copy(
            inputs[index].at[:, rows_of(q), :], landing(index, b), load_own.at[index]
        )

    for index in range(6):
        for shift in range(1, group):
            load_copy(index, shift, b, (b + shift) % group).start()
        own_copy(index).start()

    def wait_load(index):
        own_copy(index).wait()
        for shift in range(1, group):
            load_copy(index, shift, (b + group - shift) % group, b).wait_recv()

    def clear(where, value):
        for kind in range(2):
            for slot in range(2):
                field[(kind, slot) + where] = jnp.zeros(value, jnp.float32)

    @pl.when(a == 0)
    def _():
        clear((slice(0, HALO), slice(ROWS, ROWS + height)), (HALO, height, breadth))

    @pl.when(a == outer - 1)
    def _():
        clear(
            (slice(HALO + layers, 2 * HALO + layers), slice(ROWS, ROWS + height)),
            (HALO, height, breadth),
        )

    @pl.when(q == 0)
    def _():
        clear((slice(HALO, HALO + layers), slice(0, ROWS)), (layers, ROWS, breadth))

    @pl.when(q == group - 1)
    def _():
        clear(
            (slice(HALO, HALO + layers), slice(ROWS + height, 2 * ROWS + height)),
            (layers, ROWS, breadth),
        )

    snaps[...] = jnp.zeros(snaps.shape, jnp.float32)

    body = pl.ds(HALO, layers)
    to_next = (a < outer - 1, a > 0, q < group - 1, q > 0)
    from_prior = (a > 0, a < outer - 1, q > 0, q < group - 1)
    partner = (
        me + group,
        me - group,
        a * group + (2 * group - q - 1) % group,
        a * group + (group - q + 1) % group,
    )

    def halo_copy(kind, way, slot):
        view = field.at[kind, slot]
        source, target = (
            (view.at[pl.ds(layers, HALO), inner], view.at[pl.ds(0, HALO), inner]),
            (view.at[pl.ds(HALO, HALO), inner], view.at[pl.ds(HALO + layers, HALO), inner]),
            (view.at[body, pl.ds(ROWS + height - HALO, HALO)], view.at[body, pl.ds(ROWS - HALO, HALO)]),
            (view.at[body, pl.ds(ROWS, HALO)], view.at[body, pl.ds(ROWS + height, HALO)]),
        )[way]
        return pltpu.make_async_remote_copy(
            src_ref=source,
            dst_ref=target,
            send_sem=halo_send.at[kind, way, slot],
            recv_sem=halo_recv.at[kind, way, slot],
            device_id={"gz": partner[way]},
            device_id_type=MESH,
        )

    def send_halo(kind, way, slot, also=None):
        allowed = to_next[way] if also is None else jnp.logical_and(to_next[way], also)

        @pl.when(allowed)
        def _():
            halo_copy(kind, way, slot).start()

    def wait_halo(kind, way, slot):
        @pl.when(from_prior[way])
        def _():
            halo_copy(kind, way, slot).wait_recv()

    def wait_sent(kind, way, slot):
        @pl.when(to_next[way])
        def _():
            halo_copy(kind, way, slot).wait_send()

    lane = lax.broadcasted_iota(jnp.int32, (1, 1, breadth), 2)
    outside = (lane < 4) | (lane >= breadth - 4)

    def advance(kind, window, local, step, now, later, chunk, top):
        base = chunk * CHUNK
        planes = pl.ds(HALO + base, CHUNK)
        center = field[kind, now, planes, inner, :]
        flat = center.reshape(CHUNK * height, breadth)
        high = flat.astype(jnp.bfloat16)
        low = (flat - high.astype(jnp.float32)).astype(jnp.bfloat16)
        lateral = jnp.dot(
            jnp.concatenate([high, low], axis=1),
            weights_a[...],
            preferred_element_type=jnp.float32,
        ) + jnp.dot(high, weights_b[...], preferred_element_type=jnp.float32)
        summed = lateral.reshape(CHUNK, height, breadth)
        for offset in range(1, 5):
            summed = summed + stencil_weights[offset] * (
                (
                    field[kind, now, pl.ds(HALO + base + offset, CHUNK), inner, :]
                    + field[kind, now, pl.ds(HALO + base - offset, CHUNK), inner, :]
                )
                + (
                    field[kind, now, planes, pl.ds(ROWS + offset, height), :]
                    + field[kind, now, planes, pl.ds(ROWS - offset, height), :]
                )
            )
        previous = field[kind, later, planes, inner, :]
        updated = 2.0 * center - previous + factor[pl.ds(base, CHUNK)] * summed
        if kind == 0:
            placed = edges[pl.ds(base, CHUNK)].reshape(CHUNK * height, breadth)
            placed = pltpu.roll(placed, lax.rem(breadth - 8 * step, breadth), 1)
            updated = jnp.where(outside, placed.reshape(CHUNK, height, breadth), updated)
        elif top:
            updated = jnp.concatenate([updated[:1] + traces[step][None], updated[1:]], axis=0)
        field[kind, later, planes, inner, :] = updated
        held = snaps[window, kind, pl.ds(base, CHUNK)]
        take = phase_ref[window] == local
        snaps[window, kind, pl.ds(base, CHUNK)] = jnp.where(take, updated, held)

    chunks = layers // CHUNK

    def whole_step(kind, window, local):
        step = window * SNAP_EVERY + local
        now = lax.rem(step, 2)
        later = 1 - now
        more = step < STEPS - 1
        run = functools.partial(advance, kind, window, local, step, now, later)
        for way in range(4):
            wait_halo(kind, way, now)
        run(0, True)
        send_halo(kind, 1, later, more)
        run(chunks - 1, False)
        send_halo(kind, 0, later, more)

        def middle(chunk, carried):
            run(chunk, False)
            return carried

        lax.fori_loop(1, chunks - 1, middle, 0)
        send_halo(kind, 2, later, more)
        send_halo(kind, 3, later, more)
        for way in range(4):
            wait_sent(kind, way, now)

    def strip_copy(window, index, sender):
        target = q * outer + index
        first = pl.multiple_of(index * strip // ROWS * ROWS, ROWS)
        return (
            snaps.at[window, :, :, pl.ds(first, ROWS), :],
            strips_out.at[window, :, pl.ds(sender * layers, layers)],
            target,
        )

    def strip_remote(window, index, sender):
        source, landed, target = strip_copy(window, index, sender)
        return pltpu.make_async_remote_copy(
            src_ref=source,
            dst_ref=landed,
            send_sem=strip_send.at[window, index],
            recv_sem=strip_recv.at[window, sender],
            device_id={"gz": target},
            device_id_type=MESH,
        )

    def strip_local(window, index):
        source, landed, _ = strip_copy(window, index, a)
        return pltpu.make_async_copy(source, landed, strip_own.at[window])

    def start_strip(window, turn):
        index = (turn + a) % outer
        target = q * outer + index

        @pl.when(jnp.logical_and(target != me, turn < outer))
        def _():
            strip_remote(window, index, a).start()

        @pl.when(jnp.logical_and(target == me, turn < outer))
        def _():
            strip_local(window, index).start()

    def finish_strips(window):
        for turn in range(outer):
            index = (turn + a) % outer
            target = q * outer + index

            @pl.when(target != me)
            def _():
                strip_remote(window, index, a).wait_send()

            @pl.when(target == me)
            def _():
                strip_local(window, index).wait()

        quarter = me // outer
        for sender in range(outer):

            @pl.when(sender * group + (group - quarter) % group != me)
            def _():
                strip_remote(window, 0, sender).wait_recv()

    for index in (0, 1):
        wait_load(index)
    for way in range(4):
        send_halo(1, way, 0)
    for index in (3,):
        wait_load(index)
    for way in range(4):
        send_halo(0, way, 0)
    for index in (2, 4, 5):
        wait_load(index)
    for index in range(6):
        for shift in range(1, group):
            load_copy(index, shift, b, (b + shift) % group).wait_send()

    share = (outer + SNAP_EVERY - 1) // SNAP_EVERY
    for window in range(SNAPS):

        def both(local, carried):
            whole_step(1, window, local)
            whole_step(0, window, local)
            if window > 0:
                for part in range(share):
                    start_strip(window - 1, local * share + part)
            return carried

        lax.fori_loop(0, SNAP_EVERY, both, 0)
    for turn in range(outer):
        start_strip(SNAPS - 1, turn)

    last = STEPS % 2
    outs = (src_out, rec_out)

    def back_parts(kind, sender, target):
        return (
            field.at[kind, last, pl.ds(HALO + target * thin, thin), inner],
            outs[kind].at[:, rows_of((group - sender) % group), :],
        )

    def back_copy(kind, shift, sender, target):
        source, landed = back_parts(kind, sender, target)
        return pltpu.make_async_remote_copy(
            src_ref=source,
            dst_ref=landed,
            send_sem=back_send.at[kind, shift],
            recv_sem=back_recv.at[kind, shift],
            device_id={"gz": a * group + target},
            device_id_type=MESH,
        )

    def back_local(kind):
        source, landed = back_parts(kind, b, b)
        return pltpu.make_async_copy(source, landed, back_own.at[kind])

    for kind in range(2):
        back_local(kind).start()
        for shift in range(1, group):
            back_copy(kind, shift, b, (b + shift) % group).start()
    for kind in range(2):
        back_local(kind).wait()
        for shift in range(1, group):
            back_copy(kind, shift, b, (b + shift) % group).wait_send()
            back_copy(kind, shift, (b + group - shift) % group, b).wait_recv()
    for window in range(SNAPS):
        finish_strips(window)


def image_kernel(lag_ref, pivot_ref, strips, image, inverse):
    depth = strips.shape[2]
    breadth = strips.shape[4]
    lags = image.shape[0]
    unit = strips.shape[3:]

    def down(z, carried):
        first = strips[0, 0, z]
        second = strips[1, 0, z]
        value = (first * first + second * second + smoothing * carried) * pivot_ref[z]
        inverse[z] = value
        return value

    lax.fori_loop(0, depth, down, jnp.zeros(unit, jnp.float32), unroll=8)

    def up(turn, carried):
        z = depth - 1 - turn
        value = inverse[z] + (smoothing * pivot_ref[z]) * carried
        inverse[z] = 1.0 / (value + damping)
        return value

    lax.fori_loop(0, depth, up, jnp.zeros(unit, jnp.float32), unroll=8)

    lane = lax.broadcasted_iota(jnp.int32, unit, 1)
    some = 32
    for index in range(lags):
        lag = lag_ref[index]
        reach = jnp.abs(lag)
        inside = (lane >= reach) & (lane < breadth - reach)
        back = lax.rem(2 * breadth - 2 * lag, breadth)
        forth = lax.rem(breadth + lag, breadth)

        def layers(block, carried):
            z = pl.ds(block * some, some)
            raw = strips[0, 0, z] * pltpu.roll(strips[0, 1, z], back, 2)
            raw = raw + strips[1, 0, z] * pltpu.roll(strips[1, 1, z], back, 2)
            raw = jnp.where(inside[None], pltpu.roll(raw, forth, 2), 0.0)
            image[index, z] = (raw * inverse[z]).astype(jnp.bfloat16)
            return carried

        lax.fori_loop(0, depth // some, layers, 0)


def local(
    count,
    source_now,
    source_before,
    receiver_now,
    receiver_before,
    speed_term,
    saved_faces,
    face_steps,
    traces,
    lag_offsets,
    snap_phase,
):
    thin, wide, breadth = source_now.shape
    group = 4
    outer = count // group
    layers = thin * group
    depth = thin * count
    height = wide // group
    strip = wide // count
    me = lax.axis_index("gz")

    ordered = jnp.take(saved_faces, face_steps, axis=0)
    ordered = jnp.concatenate([ordered[:, 4:], ordered[:, :4]], axis=1)
    ordered = ordered.reshape(STEPS * 8, thin * wide).T.reshape(thin, wide, STEPS * 8)
    faces = jnp.pad(ordered, ((0, 0), (0, 0), (0, breadth - STEPS * 8)))
    faces = jnp.concatenate([faces[:, :, 4:], faces[:, :, :4]], axis=2)

    rows = lax.dynamic_slice_in_dim(traces, (group - me % group) % group * height, height, 1)
    top = jnp.where(me // group == 0, rows.astype(jnp.float32), 0.0)
    weights_a, weights_b = lateral_weights(breadth)

    any_space = pl.BlockSpec(memory_space=pl.ANY)
    vmem = pl.BlockSpec(memory_space=pltpu.VMEM)
    smem = pl.BlockSpec(memory_space=pltpu.SMEM)
    dma = pltpu.SemaphoreType.DMA
    flat = jax.ShapeDtypeStruct(source_now.shape, jnp.float32)
    strips, source_final, receiver_final = pl.pallas_call(
        functools.partial(wave_kernel, count, group, strip),
        out_shape=(
            jax.ShapeDtypeStruct((SNAPS, 2, depth, ROWS, breadth), jnp.float32),
            flat,
            flat,
        ),
        in_specs=[smem] + [any_space] * 6 + [vmem] * 3,
        out_specs=(any_space, any_space, any_space),
        scratch_shapes=[
            pltpu.VMEM((2, 2, layers + 2 * HALO, height + 2 * ROWS, breadth), jnp.float32),
            pltpu.VMEM((layers, height, breadth), jnp.float32),
            pltpu.VMEM((layers, height, breadth), jnp.float32),
            pltpu.VMEM((SNAPS, 2, layers, height, breadth), jnp.float32),
            dma((6, group)),
            dma((6, group)),
            dma((6,)),
            dma((2, 4, 2)),
            dma((2, 4, 2)),
            dma((SNAPS, outer)),
            dma((SNAPS, outer)),
            dma((SNAPS,)),
            dma((2, group)),
            dma((2, group)),
            dma((2,)),
        ],
        compiler_params=pltpu.CompilerParams(
            has_side_effects=True, vmem_limit_bytes=40 * 1024 * 1024
        ),
        name="waves",
    )(
        snap_phase,
        source_now,
        source_before,
        receiver_now,
        receiver_before,
        speed_term,
        faces,
        top,
        weights_a,
        weights_b,
    )

    if strip < ROWS:
        strips = lax.dynamic_slice_in_dim(strips, (me * strip) % ROWS, strip, 3)
    pivots = []
    pivot = 0.0
    for _ in range(depth):
        pivot = 1.0 / (1.0 + 2.0 * smoothing - smoothing * smoothing * pivot)
        pivots.append(pivot)
    image = pl.pallas_call(
        image_kernel,
        out_shape=jax.ShapeDtypeStruct(
            (lag_offsets.shape[0], depth, strip, breadth), jnp.bfloat16
        ),
        in_specs=[smem, smem, vmem],
        out_specs=vmem,
        scratch_shapes=[pltpu.VMEM((depth, strip, breadth), jnp.float32)],
        compiler_params=pltpu.CompilerParams(vmem_limit_bytes=48 * 1024 * 1024),
        name="images",
    )(lag_offsets, jnp.asarray(np.array(pivots, np.float32)), strips)
    return image, source_final, receiver_final


def solution(mesh):
    return jax.shard_map(
        functools.partial(local, mesh.shape["gz"]),
        mesh=mesh,
        in_specs=(
            P(("shot", "gz"), None, None),
            P(("shot", "gz"), None, None),
            P(("shot", "gz"), None, None),
            P(("shot", "gz"), None, None),
            P("gz", None, None),
            P("shot", None, "gz", None),
            P(),
            P("shot", None, None),
            P(),
            P(),
        ),
        out_specs=(
            P("shot", None, "gz", None),
            P(("shot", "gz"), None, None),
            P(("shot", "gz"), None, None),
        ),
        check_vma=False,
    )
```

profile of v0, /device:TPU:29, one launch (start us, length us, event | category | flops | bytes accessed | tf_op | source)
XLA Modules:
  0.0 183.7 jit_solution(10322908938672556809)
XLA Ops:
  0.6 0.0 copy-start
  0.7 0.7 compare_and_fusion
  1.4 0.7 compare_select_fusion
  2.1 0.9 convert_select_fusion.traces
  3.0 0.0 copy-done
  3.0 0.6 gather_fusion
  3.6 0.1 broadcast_select_fusion
  3.7 0.0 copy-start.1
  3.7 0.0 copy-start.2
  3.8 0.0 copy-start.3
  3.8 0.0 copy-start.4
  3.8 0.0 copy-start.5
  3.8 0.0 copy-start.6
  3.8 0.0 copy-start.7
  3.8 0.0 copy-start.8
  3.8 0.8 copy.18
  4.7 2.1 %copy.15 = f32[96,1024]{0,1:T(8,128)} copy(f32[96,1024]{1,0:T(8,128)} %bitcast.12) | data formatting | bytes 786432 | tf_op jit(solution)/shard_map/reshape | solution.py:451
  6.7 1.2 pad_slice_fusion
  8.0 1.2 pad_maximum_fusion.faces
  9.2 0.0 copy-done.1
  9.2 0.0 copy-done.2
  9.2 0.0 copy-done.3
  9.2 0.0 copy-done.4
  9.2 0.0 copy-done.5
  9.3 0.0 copy-done.6
  9.3 0.0 copy-done.7
  9.3 0.0 copy-done.8
  9.3 0.0 copy-start.9
  9.3 0.0 copy-start.10
  9.3 162.7 %waves.1 = (f32[2,2,128,8,128]{4,3,2,1,0:T(8,128)S(1)}, f32[8,128,128]{2,1,0:T(8,128)S(1)}, f32[8,128,128]{2,1,0:T(8,128)S(1)}) custom-call(s32[2]{0:T(128)S(1)} %copy-done.8, f32[8,128,128]{2,1,0:T(8,128)S(1)} %copy-done.1, f32[8,128,128]{2,1,0:T(8,128)S(1)} %copy-done.2, f32[8,128,128]{2,1,0:T(8,128)S(1)} %copy-done.3, f32[8,128,128]{2,1,0:T(8,128)S(1)} %copy-done.4, ...), custom_call_target="tpu_custom_call" | custom-call | tf_op jit(solution)/shard_map/waves/pallas_call | solution.py:464
  172.0 0.0 copy-done.9
  172.0 0.0 copy-done.10
  172.0 10.1 %images.1 = bf16[8,128,8,128]{3,2,1,0:T(8,128)(2,1)} custom-call(s32[8]{0:T(128)S(1)} %copy-done.9, f32[128]{0:T(128)S(1)} %copy-done.10, f32[2,2,128,8,128]{4,3,2,1,0:T(8,128)S(1)} %get-tuple-element.6.strips), custom_call_target="tpu_custom_call" | custom-call | tf_op jit(solution)/shard_map/images/pallas_call | solution.py:514
  182.1 0.8 copy.21
  182.9 0.8 copy.22
  (3 shorter events, 0.1 us)
Async XLA Ops:
  0.6 2.3 %copy-start = (f32[12,8,8,128]{3,2,1,0:T(8,128)S(1)}, f32[12,8,8,128]{3,2,1,0:T(8,128)}, u32[]{:S(2)}) copy-start(f32[12,8,8,128]{3,2,1,0:T(8,128)} %param.17) | copy-start | bytes 1179652
  3.7 5.5 %copy-start.1 = (f32[8,128,128]{2,1,0:T(8,128)S(1)}, f32[8,128,128]{2,1,0:T(8,128)}, u32[]{:S(2)}) copy-start(f32[8,128,128]{2,1,0:T(8,128)} %src_now.1) | copy-start | bytes 1572868
  3.7 5.5 %copy-start.2 = (f32[8,128,128]{2,1,0:T(8,128)S(1)}, f32[8,128,128]{2,1,0:T(8,128)}, u32[]{:S(2)}) copy-start(f32[8,128,128]{2,1,0:T(8,128)} %src_old.1) | copy-start | bytes 1572868
  3.8 5.5 %copy-start.3 = (f32[8,128,128]{2,1,0:T(8,128)S(1)}, f32[8,128,128]{2,1,0:T(8,128)}, u32[]{:S(2)}) copy-start(f32[8,128,128]{2,1,0:T(8,128)} %rec_now.1) | copy-start | bytes 1572868
  3.8 5.5 %copy-start.4 = (f32[8,128,128]{2,1,0:T(8,128)S(1)}, f32[8,128,128]{2,1,0:T(8,128)}, u32[]{:S(2)}) copy-start(f32[8,128,128]{2,1,0:T(8,128)} %rec_old.1) | copy-start | bytes 1572868
  3.8 5.5 %copy-start.5 = (f32[8,128,128]{2,1,0:T(8,128)S(1)}, f32[8,128,128]{2,1,0:T(8,128)}, u32[]{:S(2)}) copy-start(f32[8,128,128]{2,1,0:T(8,128)} %speed.1) | copy-start | bytes 1572868
  3.8 5.5 %copy-start.6 = (bf16[256,128]{1,0:T(8,128)(2,1)S(1)}, bf16[256,128]{1,0:T(8,128)(2,1)}, u32[]{:S(2)}) copy-start(bf16[256,128]{1,0:T(8,128)(2,1)} %constant.72.weights_a) | copy-start | bytes 196612
  3.8 5.5 %copy-start.7 = (bf16[128,128]{1,0:T(8,128)(2,1)S(1)}, bf16[128,128]{1,0:T(8,128)(2,1)}, u32[]{:S(2)}) copy-start(bf16[128,128]{1,0:T(8,128)(2,1)} %constant.75.weights_b) | copy-start | bytes 98308
  3.8 5.5 %copy-start.8 = (s32[2]{0:T(128)S(1)}, s32[2]{0:T(128)}, u32[]{:S(2)}) copy-start(s32[2]{0:T(128)} %phase_ref.1) | copy-start | bytes 28
  9.3 162.7 %copy-start.9 = (s32[8]{0:T(128)S(1)}, s32[8]{0:T(128)}, u32[]{:S(2)}) copy-start(s32[8]{0:T(128)} %lag_ref.1) | copy-start | bytes 100
  9.3 162.7 %copy-start.10 = (f32[128]{0:T(128)S(1)}, f32[128]{0:T(128)}, u32[]{:S(2)}) copy-start(f32[128]{0:T(128)} %constant.62.clone.pivot_ref) | copy-start | bytes 1540
where the time goes:
time: 184 us
  Pallas kernels  173 us (94%)
  local copies, waits for them, and re-layouts  6.38 us (3%)
  other arithmetic  3.65 us (2%)
    pallas_call x1, Pallas kernels, local(): pl.pallas_call(functools.partial(wave_kernel, count, group, strip), out_s...  163 us
    pallas_call x1, Pallas kernels, local(): pl.pallas_call(image_kernel, out_shape=jax.ShapeDtypeStruct((lag_offsets....  10.1 us

commit v1 on v0

v1 whole, which is shorter than its diff:
```python
import functools

import jax
import jax.numpy as jnp
import numpy as np
from jax import lax
from jax.experimental import pallas as pl
from jax.experimental.pallas import tpu as pltpu
from jax.sharding import PartitionSpec as P

SNAP_EVERY = 6
SNAPS = 2
STEPS = SNAPS * SNAP_EVERY
HALO = 4
ROWS = 8
CHUNK = 4
GROUP = 4
PIECES = 4
EPOCH = 4
EPOCHS = STEPS // EPOCH

stencil_weights = (-205.0 / 72.0, 8.0 / 5.0, -1.0 / 5.0, 8.0 / 315.0, -1.0 / 560.0)
damping = 0.25
smoothing = 16.0
MESH = pl.DeviceIdType.MESH


def lateral_weights(breadth):
    apart = np.abs(np.arange(breadth)[:, None] - np.arange(breadth)[None, :])
    band = np.zeros((breadth, breadth), np.float64)
    band[apart == 0] = 3.0 * stencil_weights[0]
    for offset in range(1, 5):
        band[apart == offset] = stencil_weights[offset]
    band = jnp.asarray(band, jnp.float32)
    high = band.astype(jnp.bfloat16)
    low = (band - high.astype(jnp.float32)).astype(jnp.bfloat16)
    return jnp.concatenate([high, high], axis=0), low


def wave_kernel(
    count,
    strip,
    phase_ref,
    order_ref,
    src_now,
    src_old,
    rec_now,
    rec_old,
    speed,
    faces,
    traces,
    weights_a,
    weights_b,
    strips_out,
    src_out,
    rec_out,
    field,
    factor,
    packed,
    edges,
    halo,
    snaps,
    load_send,
    load_recv,
    load_own,
    edge_send,
    edge_recv,
    z_send,
    z_recv,
    row_send,
    row_recv,
    strip_send,
    strip_recv,
    strip_own,
    back_send,
    back_recv,
    back_own,
):
    me = lax.axis_index("gz")
    outer = count // GROUP
    a = me // GROUP
    b = me % GROUP
    kind = b // 2
    c = b % 2
    thin = src_now.shape[0]
    layers = thin * GROUP
    height = src_now.shape[1] // 2
    breadth = src_now.shape[2]
    inner = pl.ds(ROWS, height)
    now_of = (src_now, rec_now)
    old_of = (src_old, rec_old)
    outs = (src_out, rec_out)

    def load_refs(index, target, sender):
        rows = pl.ds(target % 2 * height, height)
        planes = pl.ds(HALO + sender * thin, thin)
        source = (speed, now_of[target // 2], old_of[target // 2])[index]
        landed = (
            factor.at[pl.ds(sender * thin, thin)],
            field.at[0, planes, inner],
            field.at[1, planes, inner],
        )[index]
        return source.at[:, rows, :], landed

    def load_remote(index, target, sender):
        source, landed = load_refs(index, target, sender)
        return pltpu.make_async_remote_copy(
            src_ref=source,
            dst_ref=landed,
            send_sem=load_send.at[index, target],
            recv_sem=load_recv.at[index, sender],
            device_id={"gz": a * GROUP + target},
            device_id_type=MESH,
        )

    def load_local(index, target):
        source, landed = load_refs(index, target, target)
        return pltpu.make_async_copy(source, landed, load_own.at[index])

    for index in range(3):
        for target in range(GROUP):

            @pl.when(b != target)
            def _():
                load_remote(index, target, b).start()

    for index in range(3):
        for target in range(GROUP):

            @pl.when(b == target)
            def _():
                load_local(index, target).start()

    def wait_load(index):
        for sender in range(GROUP):

            @pl.when(b == sender)
            def _():
                load_local(index, sender).wait()

            @pl.when(b != sender)
            def _():
                load_remote(index, sender, sender).wait_recv()

    lane = lax.broadcasted_iota(jnp.int32, (1, 1, breadth), 2)
    across = 8 * EPOCH
    groups = breadth // across
    tall = height // groups
    for z in range(thin):
        parts = [
            pltpu.roll(faces[order_ref[step], :, z, :], 4, 0) for step in range(STEPS)
        ]
        parts.append(jnp.zeros((breadth - 8 * STEPS, 2 * height), jnp.float32))
        turned = jnp.concatenate(parts, axis=0).T
        for epoch in range(EPOCHS):
            for half in range(2):
                block = None
                for part in range(groups):
                    first = half * height + part * tall
                    moved = turned[first : first + tall]
                    turn = (across * (part - epoch)) % breadth
                    if turn:
                        moved = pltpu.roll(moved, turn, 1)
                    if block is None:
                        block = moved
                    else:
                        block = jnp.where(lane[0] >= across * part, moved, block)
                packed[epoch, half, z] = block

    def edge_remote(epoch, target, sender):
        return pltpu.make_async_remote_copy(
            src_ref=packed.at[epoch, target],
            dst_ref=edges.at[epoch, pl.ds(sender * thin, thin)],
            send_sem=edge_send.at[epoch, target],
            recv_sem=edge_recv.at[epoch, sender],
            device_id={"gz": a * GROUP + target},
            device_id_type=MESH,
        )

    for epoch in range(EPOCHS):
        for target in range(2):

            @pl.when(b != target)
            def _():
                edge_remote(epoch, target, b).start()

            @pl.when(b == target)
            def _():
                edges[epoch, pl.ds(target * thin, thin)] = packed[epoch, target]

    def wait_edge(epoch):
        for sender in range(GROUP):

            @pl.when(jnp.logical_and(kind == 0, b != sender))
            def _():
                edge_remote(epoch, 0, sender).wait_recv()

    for slot in range(2):
        for first in (0, HALO + layers):
            field[slot, pl.ds(first, HALO), inner] = jnp.zeros(
                (HALO, height, breadth), jnp.float32
            )

        @pl.when(c == 0)
        def _():
            field[slot, pl.ds(HALO, layers), pl.ds(0, ROWS)] = jnp.zeros(
                (layers, ROWS, breadth), jnp.float32
            )

        @pl.when(c == 1)
        def _():
            field[slot, pl.ds(HALO, layers), pl.ds(ROWS + height, ROWS)] = jnp.zeros(
                (layers, ROWS, breadth), jnp.float32
            )

        @pl.when(a == 0)
        def _():
            halo[0, slot] = jnp.zeros((HALO, height, breadth), jnp.float32)

        @pl.when(a == outer - 1)
        def _():
            halo[1, slot] = jnp.zeros((HALO, height, breadth), jnp.float32)

    snaps[...] = jnp.zeros(snaps.shape, jnp.float32)

    span = height // PIECES
    present = (a > 0, a < outer - 1)

    def z_copy(side, piece, slot):
        return pltpu.make_async_remote_copy(
            src_ref=field.at[
                slot,
                pl.ds((HALO, layers)[side], HALO),
                pl.ds(ROWS + piece * span, span),
            ],
            dst_ref=halo.at[1 - side, slot, :, pl.ds(piece * span, span)],
            send_sem=z_send.at[side, slot, piece],
            recv_sem=z_recv.at[1 - side, slot, piece],
            device_id={"gz": (me - GROUP, me + GROUP)[side]},
            device_id_type=MESH,
        )

    def send_z(piece, slot, also=None):
        for side in range(2):
            allowed = present[side]
            if also is not None:
                allowed = jnp.logical_and(allowed, also)

            @pl.when(allowed)
            def _():
                z_copy(side, piece, slot).start()

    def wait_z(piece, slot):
        for side in range(2):

            @pl.when(present[side])
            def _():
                z_copy(1 - side, piece, slot).wait_recv()

    def sent_z(slot):
        for side in range(2):

            @pl.when(present[side])
            def _():
                for piece in range(PIECES):
                    z_copy(side, piece, slot).wait_send()

    body = pl.ds(HALO, layers)

    def row_copy(way, slot):
        first, landed = (
            (ROWS + height - HALO, ROWS - HALO),
            (ROWS, ROWS + height),
        )[way]
        return pltpu.make_async_remote_copy(
            src_ref=field.at[slot, body, pl.ds(first, HALO)],
            dst_ref=field.at[slot, body, pl.ds(landed, HALO)],
            send_sem=row_send.at[slot],
            recv_sem=row_recv.at[slot],
            device_id={"gz": me + 1 - 2 * c},
            device_id_type=MESH,
        )

    def each_way(do, also=None):
        for way in range(2):
            allowed = c == way
            if also is not None:
                allowed = jnp.logical_and(allowed, also)

            @pl.when(allowed)
            def _():
                do(way)

    def send_row(slot, also=None):
        each_way(lambda way: row_copy(way, slot).start(), also)

    def wait_row(slot):
        each_way(lambda way: row_copy(1 - way, slot).wait_recv())

    def sent_row(slot):
        each_way(lambda way: row_copy(way, slot).wait_send())

    outside = ((lane < 4) | (lane >= breadth - 4)) & (kind == 0)
    lit = jnp.logical_and(a == 0, kind == 1)

    def partial(step, now, later, base, top):
        planes = pl.ds(HALO + base, CHUNK)
        center = field[now, planes, inner, :]
        flat = center.reshape(CHUNK * height, breadth)
        high = flat.astype(jnp.bfloat16)
        low = (flat - high.astype(jnp.float32)).astype(jnp.bfloat16)
        lateral = jnp.dot(
            jnp.concatenate([high, low], axis=1),
            weights_a[...],
            preferred_element_type=jnp.float32,
        ) + jnp.dot(high, weights_b[...], preferred_element_type=jnp.float32)
        summed = lateral.reshape(CHUNK, height, breadth)
        for offset in range(1, 5):
            summed = summed + stencil_weights[offset] * (
                (
                    field[now, pl.ds(HALO + base + offset, CHUNK), inner, :]
                    + field[now, pl.ds(HALO + base - offset, CHUNK), inner, :]
                )
                + (
                    field[now, planes, pl.ds(ROWS + offset, height), :]
                    + field[now, planes, pl.ds(ROWS - offset, height), :]
                )
            )
        previous = field[later, planes, inner, :]
        updated = 2.0 * center - previous + factor[pl.ds(base, CHUNK)] * summed
        edge = edges[step // EPOCH, pl.ds(base, CHUNK)].reshape(CHUNK * tall, breadth)
        placed = jnp.concatenate(
            [
                pltpu.roll(
                    edge,
                    lax.rem(
                        3 * breadth - 4 - across * part - 8 * (step % EPOCH), breadth
                    ),
                    1,
                ).reshape(CHUNK, tall, breadth)
                for part in range(groups)
            ],
            axis=1,
        )
        updated = jnp.where(outside, placed, updated)
        if top:
            trace = traces[step, pl.ds(pl.multiple_of(c * height, height), height)]
            trace = jnp.where(lit, trace.astype(jnp.float32), 0.0)
            updated = jnp.concatenate([updated[:1] + trace[None], updated[1:]], axis=0)
        return updated

    def keep(window, take, base, rows, value):
        held = snaps[window, pl.ds(base, value.shape[0]), rows]
        snaps[window, pl.ds(base, value.shape[0]), rows] = jnp.where(take, value, held)

    def complete(window, take, now, later, piece):
        rows = pl.ds(piece * span, span)
        wide = pl.ds(ROWS + piece * span, span)
        for side in range(2):
            base = (0, layers - HALO)[side]
            held = [halo[side, now, near, rows] for near in range(HALO)]
            added = []
            for near in range(HALO):
                total = None
                reach = HALO - near if side == 0 else near + 1
                for k in range(reach):
                    offset = HALO - k
                    index = near + k if side == 0 else near - k
                    term = stencil_weights[offset] * held[index]
                    total = term if total is None else total + term
                added.append(total[None])
            added = jnp.concatenate(added, axis=0)
            planes = pl.ds(HALO + base, HALO)
            value = (
                field[later, planes, wide] + factor[pl.ds(base, HALO), rows] * added
            )
            field[later, planes, wide] = value
            keep(window, take, base, rows, value)

    whole = pl.ds(0, height)

    def whole_step(window, local):
        step = window * SNAP_EVERY + local
        now = lax.rem(step, 2)
        later = 1 - now
        more = step < STEPS - 1
        take = phase_ref[window] == local

        @pl.when(lax.rem(step, EPOCH) == 0)
        def _():
            wait_edge(step // EPOCH)

        wait_row(now)
        for base, top in ((0, True), (layers - HALO, False)):
            field[later, pl.ds(HALO + base, CHUNK), inner] = partial(
                step, now, later, base, top
            )
        for piece in range(PIECES):
            wait_z(piece, now)
            complete(window, take, now, later, piece)
            send_z(piece, later, more)

        def middle(chunk, carried):
            base = chunk * CHUNK
            value = partial(step, now, later, base, False)
            field[later, pl.ds(HALO + base, CHUNK), inner] = value
            keep(window, take, base, whole, value)
            return carried

        lax.fori_loop(1, layers // CHUNK - 1, middle, 0)
        send_row(later, more)
        sent_z(now)
        sent_row(now)

    half = count // 2

    def strip_refs(window, index):
        first = pl.multiple_of(index * strip // ROWS * ROWS, ROWS)
        return (
            snaps.at[window, :, pl.ds(first, ROWS), :],
            strips_out.at[window, kind, pl.ds(a * layers, layers)],
        )

    def strip_remote(window, index, sender, sort):
        source = snaps.at[
            window, :, pl.ds(pl.multiple_of(index * strip // ROWS * ROWS, ROWS), ROWS), :
        ]
        return pltpu.make_async_remote_copy(
            src_ref=source,
            dst_ref=strips_out.at[window, sort, pl.ds(sender * layers, layers)],
            send_sem=strip_send.at[window, index],
            recv_sem=strip_recv.at[window, sort, sender],
            device_id={"gz": c * half + index},
            device_id_type=MESH,
        )

    def strip_local(window, index):
        source, landed = strip_refs(window, index)
        return pltpu.make_async_copy(source, landed, strip_own.at[window])

    def start_strip(window, turn):
        index = (turn + GROUP * a + 2 * kind) % half
        target = c * half + index

        @pl.when(jnp.logical_and(target != me, turn < half))
        def _():
            strip_remote(window, index, a, kind).start()

        @pl.when(jnp.logical_and(target == me, turn < half))
        def _():
            strip_local(window, index).start()

    def finish_strips(window):
        def sent(index, carried):
            target = c * half + index

            @pl.when(target != me)
            def _():
                strip_remote(window, index, a, kind).wait_send()

            @pl.when(target == me)
            def _():
                strip_local(window, index).wait()

            return carried

        lax.fori_loop(0, half, sent, 0)
        for sort in range(2):
            for sender in range(outer):

                @pl.when(sender * GROUP + 2 * sort + me // half != me)
                def _():
                    strip_remote(window, 0, sender, sort).wait_recv()

    wait_load(1)
    for piece in range(PIECES):
        send_z(piece, 0)
    send_row(0)
    wait_load(0)

    def mask(layer, carried):
        factor[layer] = jnp.where(outside[0], 0.0, factor[layer])
        return carried

    lax.fori_loop(0, layers, mask, 0)
    wait_load(2)
    for index in range(3):
        for target in range(GROUP):

            @pl.when(b != target)
            def _():
                load_remote(index, target, b).wait_send()

    share = (half + SNAP_EVERY - 1) // SNAP_EVERY
    for window in range(SNAPS):

        def both(local, carried):
            whole_step(window, local)
            if window > 0:
                for part in range(share):
                    start_strip(window - 1, local * share + part)
            return carried

        lax.fori_loop(0, SNAP_EVERY, both, 0)
    lax.fori_loop(0, half, lambda turn, carried: (start_strip(SNAPS - 1, turn), carried)[1], 0)

    last = STEPS % 2

    def back_refs(sort, target):
        return (
            field.at[last, pl.ds(HALO + target * thin, thin), inner],
            outs[sort].at[:, pl.ds(pl.multiple_of(c * height, height), height), :],
        )

    def back_remote(sort, target):
        source, landed = back_refs(sort, target)
        return pltpu.make_async_remote_copy(
            src_ref=source,
            dst_ref=landed,
            send_sem=back_send.at[target],
            recv_sem=back_recv.at[sort, c],
            device_id={"gz": a * GROUP + target},
            device_id_type=MESH,
        )

    def back_arrival(sort, side):
        return pltpu.make_async_remote_copy(
            src_ref=field.at[last, pl.ds(HALO, thin), inner],
            dst_ref=outs[sort].at[:, pl.ds(side * height, height), :],
            send_sem=back_send.at[0],
            recv_sem=back_recv.at[sort, side],
            device_id={"gz": a * GROUP + 2 * sort + side},
            device_id_type=MESH,
        )

    def back_local(sort, target):
        source, landed = back_refs(sort, target)
        return pltpu.make_async_copy(source, landed, back_own.at[0])

    def each_back(remote, own):
        for sort in range(2):
            for target in range(GROUP):

                @pl.when(jnp.logical_and(kind == sort, b != target))
                def _():
                    remote(sort, target)

                if target // 2 == sort:

                    @pl.when(b == target)
                    def _():
                        own(sort, target)

    each_back(
        lambda sort, target: back_remote(sort, target).start(),
        lambda sort, target: back_local(sort, target).start(),
    )
    for epoch in range(EPOCHS):
        for target in range(2):

            @pl.when(b != target)
            def _():
                edge_remote(epoch, target, b).wait_send()

    each_back(
        lambda sort, target: back_remote(sort, target).wait_send(),
        lambda sort, target: back_local(sort, target).wait(),
    )
    for sort in range(2):
        for side in range(2):

            @pl.when(b != 2 * sort + side)
            def _():
                back_arrival(sort, side).wait_recv()

    for window in range(SNAPS):
        finish_strips(window)


def image_kernel(lag_ref, pivot_ref, strips, image, inverse):
    depth = strips.shape[2]
    breadth = strips.shape[4]
    lags = image.shape[0]
    unit = strips.shape[3:]

    def down(z, carried):
        first = strips[0, 0, z]
        second = strips[1, 0, z]
        value = (first * first + second * second + smoothing * carried) * pivot_ref[z]
        inverse[z] = value
        return value

    lax.fori_loop(0, depth, down, jnp.zeros(unit, jnp.float32), unroll=8)

    def up(turn, carried):
        z = depth - 1 - turn
        value = inverse[z] + (smoothing * pivot_ref[z]) * carried
        inverse[z] = 1.0 / (value + damping)
        return value

    lax.fori_loop(0, depth, up, jnp.zeros(unit, jnp.float32), unroll=8)

    lane = lax.broadcasted_iota(jnp.int32, unit, 1)
    some = 32
    for index in range(lags):
        lag = lag_ref[index]
        reach = jnp.abs(lag)
        inside = (lane >= reach) & (lane < breadth - reach)
        back = lax.rem(2 * breadth - 2 * lag, breadth)
        forth = lax.rem(breadth + lag, breadth)

        def layers(block, carried):
            z = pl.ds(block * some, some)
            raw = strips[0, 0, z] * pltpu.roll(strips[0, 1, z], back, 2)
            raw = raw + strips[1, 0, z] * pltpu.roll(strips[1, 1, z], back, 2)
            raw = jnp.where(inside[None], pltpu.roll(raw, forth, 2), 0.0)
            image[index, z] = (raw * inverse[z]).astype(jnp.bfloat16)
            return carried

        lax.fori_loop(0, depth // some, layers, 0)


def local(
    count,
    source_now,
    source_before,
    receiver_now,
    receiver_before,
    speed_term,
    saved_faces,
    face_steps,
    traces,
    lag_offsets,
    snap_phase,
):
    thin, wide, breadth = source_now.shape
    layers = thin * GROUP
    outer = count // GROUP
    half = count // 2
    depth = thin * count
    height = wide // 2
    strip = wide // count
    tall = height * 8 * EPOCH // breadth
    me = lax.axis_index("gz")
    weights_a, weights_b = lateral_weights(breadth)

    any_space = pl.BlockSpec(memory_space=pl.ANY)
    vmem = pl.BlockSpec(memory_space=pltpu.VMEM)
    smem = pl.BlockSpec(memory_space=pltpu.SMEM)
    dma = pltpu.SemaphoreType.DMA
    flat = jax.ShapeDtypeStruct(source_now.shape, jnp.float32)
    strips, source_final, receiver_final = pl.pallas_call(
        functools.partial(wave_kernel, count, strip),
        out_shape=(
            jax.ShapeDtypeStruct((SNAPS, 2, depth, ROWS, breadth), jnp.float32),
            flat,
            flat,
        ),
        in_specs=[smem] * 2 + [any_space] * 5 + [vmem] * 4,
        out_specs=(any_space, any_space, any_space),
        scratch_shapes=[
            pltpu.VMEM((2, layers + 2 * HALO, height + 2 * ROWS, breadth), jnp.float32),
            pltpu.VMEM((layers, height, breadth), jnp.float32),
            pltpu.VMEM((EPOCHS, 2, thin, tall, breadth), jnp.float32),
            pltpu.VMEM((EPOCHS, layers, tall, breadth), jnp.float32),
            pltpu.VMEM((2, 2, HALO, height, breadth), jnp.float32),
            pltpu.VMEM((SNAPS, layers, height, breadth), jnp.float32),
            dma((3, GROUP)),
            dma((3, GROUP)),
            dma((3,)),
            dma((EPOCHS, 2)),
            dma((EPOCHS, GROUP)),
            dma((2, 2, PIECES)),
            dma((2, 2, PIECES)),
            dma((2,)),
            dma((2,)),
            dma((SNAPS, half)),
            dma((SNAPS, 2, outer)),
            dma((SNAPS,)),
            dma((GROUP,)),
            dma((2, 2)),
            dma((1,)),
        ],
        compiler_params=pltpu.CompilerParams(
            has_side_effects=True, vmem_limit_bytes=40 * 1024 * 1024
        ),
        name="waves",
    )(
        snap_phase,
        face_steps,
        source_now,
        source_before,
        receiver_now,
        receiver_before,
        speed_term,
        saved_faces,
        traces,
        weights_a,
        weights_b,
    )

    if strip < ROWS:
        strips = lax.dynamic_slice_in_dim(strips, (me * strip) % ROWS, strip, 3)
    pivots = []
    pivot = 0.0
    for _ in range(depth):
        pivot = 1.0 / (1.0 + 2.0 * smoothing - smoothing * smoothing * pivot)
        pivots.append(pivot)
    image = pl.pallas_call(
        image_kernel,
        out_shape=jax.ShapeDtypeStruct(
            (lag_offsets.shape[0], depth, strip, breadth), jnp.bfloat16
        ),
        in_specs=[smem, smem, vmem],
        out_specs=vmem,
        scratch_shapes=[pltpu.VMEM((depth, strip, breadth), jnp.float32)],
        compiler_params=pltpu.CompilerParams(vmem_limit_bytes=48 * 1024 * 1024),
        name="images",
    )(lag_offsets, jnp.asarray(np.array(pivots, np.float32)), strips)
    return image, source_final, receiver_final


def solution(mesh):
    return jax.shard_map(
        functools.partial(local, mesh.shape["gz"]),
        mesh=mesh,
        in_specs=(
            P(("shot", "gz"), None, None),
            P(("shot", "gz"), None, None),
            P(("shot", "gz"), None, None),
            P(("shot", "gz"), None, None),
            P("gz", None, None),
            P("shot", None, "gz", None),
            P(),
            P("shot", None, None),
            P(),
            P(),
        ),
        out_specs=(
            P("shot", None, "gz", None),
            P(("shot", "gz"), None, None),
            P(("shot", "gz"), None, None),
        ),
        check_vma=False,
    )
```

time: 184 us -> 162 us (0.88)
  the two profiles are of different devices: /device:TPU:29 before, /device:TPU:1 now
where the time goes in v1:
time: 162 us; the launch traced here: 161 us
  Pallas kernels  149 us (92%)
  local copies, waits for them, and re-layouts  11.7 us (7%)
    pallas_call x1, Pallas kernels, local(): pl.pallas_call(functools.partial(wave_kernel, count, strip), out_shape=(j...  139 us
    unnamed x28, local copies, waits for them, and re-layouts  11.7 us
    pallas_call x1, Pallas kernels, local(): pl.pallas_call(image_kernel, out_shape=jax.ShapeDtypeStruct((lag_offsets....  10.1 us

profile of v1, /device:TPU:1, one launch (start us, length us, event | category | flops | bytes accessed | tf_op | source)
XLA Modules:
  0.0 161.3 jit_solution(4727794641129896616)
XLA Ops:
  0.6 0.0 copy-start
  0.6 1.0 copy-done
  1.7 0.0 copy-start.1
  1.7 1.0 copy-done.1
  2.7 0.0 copy-start.2
  2.7 1.0 copy-done.2
  3.8 0.0 copy-start.3
  3.8 1.0 copy-done.3
  4.8 0.0 copy-start.4
  4.8 1.0 copy-done.4
  5.8 0.0 copy-start.5
  5.8 1.0 copy-done.5
  6.8 0.0 copy-start.6
  6.8 1.0 copy-done.6
  7.8 0.0 copy-start.7
  7.8 0.8 copy-done.7
  8.7 0.0 copy-start.8
  8.7 0.8 copy-done.8
  9.4 0.0 copy-start.9
  9.4 0.7 copy-done.9
  10.1 0.0 copy-start.10
  10.1 0.7 copy-done.10
  10.7 0.0 copy-start.11
  10.8 0.0 copy-start.12
  10.8 138.9 %waves.1 = (f32[2,2,128,8,128]{4,3,2,1,0:T(8,128)S(1)}, f32[8,128,128]{2,1,0:T(8,128)S(1)}, f32[8,128,128]{2,1,0:T(8,128)S(1)}) custom-call(s32[2]{0:T(128)S(1)} %copy-done.9, s32[12]{0:T(128)S(1)} %copy-done.10, f32[8,128,128]{2,1,0:T(8,128)S(1)} %copy-done, f32[8,128,128]{2,1,0:T(8,128)S(1)} %copy-done.1, f32[8,128,128]{2,1,0:T(8,128)S(1)} %copy-done.2, ...), custom_call_target="tpu_custom_call" | custom-call | tf_op jit(solution)/shard_map/waves/pallas_call | solution.py:652
  149.6 0.0 copy-done.11
  149.6 0.0 copy-done.12
  149.7 10.1 %images.1 = bf16[8,128,8,128]{3,2,1,0:T(8,128)(2,1)} custom-call(s32[8]{0:T(128)S(1)} %copy-done.11, f32[128]{0:T(128)S(1)} %copy-done.12, f32[2,2,128,8,128]{4,3,2,1,0:T(8,128)S(1)} %get-tuple-element.6.strips), custom_call_target="tpu_custom_call" | custom-call | tf_op jit(solution)/shard_map/images/pallas_call | solution.py:709
  159.8 0.8 copy.17
  160.5 0.8 copy.18
Async XLA Ops:
  0.6 1.0 copy-start
  1.7 1.0 copy-start.1
  2.7 1.0 copy-start.2
  3.8 1.0 copy-start.3
  4.8 1.0 copy-start.4
  5.8 1.0 copy-start.5
  6.8 1.0 copy-start.6
  7.8 0.8 copy-start.7
  8.7 0.8 copy-start.8
  9.4 0.7 copy-start.9
  10.1 0.7 copy-start.10
  10.7 138.9 %copy-start.11 = (s32[8]{0:T(128)S(1)}, s32[8]{0:T(128)}, u32[]{:S(2)}) copy-start(s32[8]{0:T(128)} %lag_ref.1) | copy-start | bytes 100
  10.8 138.9 %copy-start.12 = (f32[128]{0:T(128)S(1)}, f32[128]{0:T(128)}, u32[]{:S(2)}) copy-start(f32[128]{0:T(128)} %constant.5.clone.pivot_ref) | copy-start | bytes 1540

commit v2 on v1

--- a/solution.py
+++ b/solution.py
@@ -17,6 +17,7 @@
 GROUP = 4
 PIECES = 4
 EPOCH = 4
+VMEM_BYTES = 60 * 1024 * 1024
 EPOCHS = STEPS // EPOCH
 
 stencil_weights = (-205.0 / 72.0, 8.0 / 5.0, -1.0 / 5.0, 8.0 / 315.0, -1.0 / 560.0)
@@ -26,43 +27,57 @@
 
 
 def lateral_weights(breadth):
-    apart = np.abs(np.arange(breadth)[:, None] - np.arange(breadth)[None, :])
-    band = np.zeros((breadth, breadth), np.float64)
-    band[apart == 0] = 3.0 * stencil_weights[0]
+    apart = jnp.abs(
+        lax.broadcasted_iota(jnp.int32, (breadth, breadth), 0)
+        - lax.broadcasted_iota(jnp.int32, (breadth, breadth), 1)
+    )
+    band = jnp.where(apart == 0, 3.0 * stencil_weights[0], 0.0)
     for offset in range(1, 5):
-        band[apart == offset] = stencil_weights[offset]
-    band = jnp.asarray(band, jnp.float32)
+        band = jnp.where(apart == offset, stencil_weights[offset], band)
     high = band.astype(jnp.bfloat16)
     low = (band - high.astype(jnp.float32)).astype(jnp.bfloat16)
-    return jnp.concatenate([high, high], axis=0), low
+    return high, low
 
 
 def wave_kernel(
     count,
+    shots,
     strip,
-    phase_ref,
-    order_ref,
+    lag_ref,
+    phase_hbm,
+    order_hbm,
     src_now,
     src_old,
     rec_now,
     rec_old,
     speed,
+    faces_hbm,
+    traces_hbm,
+    raw_out,
+    light_out,
+    src_out,
+    rec_out,
+    phase_ref,
+    order_ref,
     faces,
     traces,
     weights_a,
     weights_b,
-    strips_out,
-    src_out,
-    rec_out,
     field,
     factor,
     packed,
     edges,
     halo,
     snaps,
+    strips,
+    raw,
+    light,
+    small_own,
     load_send,
     load_recv,
     load_own,
+    relay_send,
+    relay_recv,
     edge_send,
     edge_recv,
     z_send,
@@ -75,6 +90,7 @@
     back_send,
     back_recv,
     back_own,
+    out_own,
 ):
     me = lax.axis_index("gz")
     outer = count // GROUP
@@ -117,13 +133,47 @@
         source, landed = load_refs(index, target, target)
         return pltpu.make_async_copy(source, landed, load_own.at[index])
 
+    paired = shots % 2 == 0
+    shot = lax.axis_index("shot")
+    parity = shot % 2
+
+    def direct(index, target):
+        if index > 0 or not paired:
+            return b != target
+        near = jnp.logical_or(kind == target // 2, parity == target % 2)
+        return jnp.logical_and(b != target, near)
+
+    def relay(sender):
+        view = factor.at[pl.ds(sender * thin, thin)]
+        return pltpu.make_async_remote_copy(
+            src_ref=view,
+            dst_ref=view,
+            send_sem=relay_send.at[sender % 2],
+            recv_sem=relay_recv.at[sender % 2],
+            device_id={"shot": shot + 1 - 2 * parity, "gz": me},
+            device_id_type=MESH,
+        )
+
+    small = (
+        (faces_hbm, faces),
+        (order_hbm, order_ref),
+        (phase_hbm, phase_ref),
+        (traces_hbm, traces),
+    )
+
+    def fetch(index):
+        source, landed = small[index]
+        return pltpu.make_async_copy(source, landed, small_own.at[index])
+
     for index in range(3):
         for target in range(GROUP):
 
-            @pl.when(b != target)
+            @pl.when(direct(index, target))
             def _():
                 load_remote(index, target, b).start()
 
+    for index in range(len(small)):
+        fetch(index).start()
     for index in range(3):
         for target in range(GROUP):
 
@@ -138,9 +188,43 @@
             def _():
                 load_local(index, sender).wait()
 
-            @pl.when(b != sender)
-            def _():
-                load_remote(index, sender, sender).wait_recv()
+            if index > 0 or not paired:
+
+                @pl.when(b != sender)
+                def _():
+                    load_remote(index, sender, sender).wait_recv()
+
+            else:
+
+                @pl.when(jnp.logical_and(b != sender, kind == sender // 2))
+                def _():
+                    load_remote(index, sender, sender).wait_recv()
+
+                @pl.when(jnp.logical_and(kind != sender // 2, parity != c))
+                def _():
+                    relay(sender).wait_recv()
+
+    def pass_on():
+        for sender in range(GROUP):
+
+            @pl.when(jnp.logical_and(kind != sender // 2, parity == c))
+            def _():
+                load_remote(0, sender, sender).wait_recv()
+                relay(sender).start()
+
+    def passed_on():
+        for sender in range(GROUP):
+
+            @pl.when(jnp.logical_and(kind != sender // 2, parity == c))
+            def _():
+                relay(sender).wait_send()
+
+    high, low = lateral_weights(breadth)
+    weights_a[pl.ds(0, breadth)] = high
+    weights_a[pl.ds(breadth, breadth)] = high
+    weights_b[...] = low
+    fetch(0).wait()
+    fetch(1).wait()
 
     lane = lax.broadcasted_iota(jnp.int32, (1, 1, breadth), 2)
     across = 8 * EPOCH
@@ -371,9 +455,8 @@
                 added.append(total[None])
             added = jnp.concatenate(added, axis=0)
             planes = pl.ds(HALO + base, HALO)
-            value = (
-                field[later, planes, wide] + factor[pl.ds(base, HALO), rows] * added
-            )
+            added = jnp.where(outside, 0.0, factor[pl.ds(base, HALO), rows] * added)
+            value = field[later, planes, wide] + added
             field[later, planes, wide] = value
             keep(window, take, base, rows, value)
 
@@ -418,7 +501,7 @@
         first = pl.multiple_of(index * strip // ROWS * ROWS, ROWS)
         return (
             snaps.at[window, :, pl.ds(first, ROWS), :],
-            strips_out.at[window, kind, pl.ds(a * layers, layers)],
+            strips.at[window, kind, pl.ds(a * layers, layers)],
         )
 
     def strip_remote(window, index, sender, sort):
@@ -427,7 +510,7 @@
         ]
         return pltpu.make_async_remote_copy(
             src_ref=source,
-            dst_ref=strips_out.at[window, sort, pl.ds(sender * layers, layers)],
+            dst_ref=strips.at[window, sort, pl.ds(sender * layers, layers)],
             send_sem=strip_send.at[window, index],
             recv_sem=strip_recv.at[window, sort, sender],
             device_id={"gz": c * half + index},
@@ -450,7 +533,7 @@
         def _():
             strip_local(window, index).start()
 
-    def finish_strips(window):
+    def sent_strips(window):
         def sent(index, carried):
             target = c * half + index
 
@@ -458,38 +541,76 @@
             def _():
                 strip_remote(window, index, a, kind).wait_send()
 
-            @pl.when(target == me)
-            def _():
-                strip_local(window, index).wait()
-
             return carried
 
         lax.fori_loop(0, half, sent, 0)
+
+    def wait_strip(window, sender):
         for sort in range(2):
-            for sender in range(outer):
-
-                @pl.when(sender * GROUP + 2 * sort + me // half != me)
-                def _():
-                    strip_remote(window, 0, sender, sort).wait_recv()
-
+            source = sender * GROUP + 2 * sort + me // half
+
+            @pl.when(source != me)
+            def _():
+                strip_remote(window, 0, sender, sort).wait_recv()
+
+            @pl.when(source == me)
+            def _():
+                strip_local(window, me % half).wait()
+
+    lags = raw.shape[0]
+    some = 16
+    unit = (ROWS, breadth)
+    column = lax.broadcasted_iota(jnp.int32, unit, 1)
+
+    def first_products(block, carried):
+        z = pl.ds(block * some, some)
+        shot_wave = strips[0, 0, z]
+        echo = strips[0, 1, z]
+        light[z] = shot_wave * shot_wave
+        for index in range(lags):
+            back = lax.rem(2 * breadth - 2 * lag_ref[index], breadth)
+            raw[index, z] = shot_wave * pltpu.roll(echo, back, 2)
+        return carried
+
+    def last_products(slab):
+        def block_products(block, carried):
+            z = pl.ds(slab * layers + block * some, some)
+            shot_wave = strips[1, 0, z]
+            echo = strips[1, 1, z]
+            light[z] = light[z] + shot_wave * shot_wave
+            for index in range(lags):
+                lag = lag_ref[index]
+                reach = jnp.abs(lag)
+                inside = (column >= reach) & (column < breadth - reach)
+                back = lax.rem(2 * breadth - 2 * lag, breadth)
+                forth = lax.rem(breadth + lag, breadth)
+                total = raw[index, z] + shot_wave * pltpu.roll(echo, back, 2)
+                raw[index, z] = jnp.where(
+                    inside[None], pltpu.roll(total, forth, 2), 0.0
+                )
+            return carried
+
+        lax.fori_loop(0, layers // some, block_products, 0)
+
+    if paired:
+        pass_on()
     wait_load(1)
     for piece in range(PIECES):
         send_z(piece, 0)
     send_row(0)
     wait_load(0)
-
-    def mask(layer, carried):
-        factor[layer] = jnp.where(outside[0], 0.0, factor[layer])
-        return carried
-
-    lax.fori_loop(0, layers, mask, 0)
     wait_load(2)
+    fetch(2).wait()
+    fetch(3).wait()
     for index in range(3):
         for target in range(GROUP):
 
-            @pl.when(b != target)
+            @pl.when(direct(index, target))
             def _():
                 load_remote(index, target, b).wait_send()
+
+    if paired:
+        passed_on()
 
     share = (half + SNAP_EVERY - 1) // SNAP_EVERY
     for window in range(SNAPS):
@@ -555,6 +676,28 @@
         lambda sort, target: back_remote(sort, target).start(),
         lambda sort, target: back_local(sort, target).start(),
     )
+    for sender in range(outer):
+        wait_strip(0, sender)
+    lax.fori_loop(0, strips.shape[2] // some, first_products, 0)
+
+    def leaving(slab, turn):
+        z = pl.ds(slab * layers, layers)
+        return (
+            pltpu.make_async_copy(light.at[z], light_out.at[z], out_own.at[0, turn]),
+            pltpu.make_async_copy(
+                raw.at[:, z], raw_out.at[:, z], out_own.at[1, turn]
+            ),
+        )
+
+    def arrivals(turn, carried):
+        slab = (a + turn) % outer
+        wait_strip(1, slab)
+        last_products(slab)
+        for leave in leaving(slab, turn):
+            leave.start()
+        return carried
+
+    lax.fori_loop(0, outer, arrivals, 0)
     for epoch in range(EPOCHS):
         for target in range(2):
 
@@ -574,54 +717,123 @@
                 back_arrival(sort, side).wait_recv()
 
     for window in range(SNAPS):
-        finish_strips(window)
-
-
-def image_kernel(lag_ref, pivot_ref, strips, image, inverse):
-    depth = strips.shape[2]
-    breadth = strips.shape[4]
-    lags = image.shape[0]
-    unit = strips.shape[3:]
-
-    def down(z, carried):
-        first = strips[0, 0, z]
-        second = strips[1, 0, z]
-        value = (first * first + second * second + smoothing * carried) * pivot_ref[z]
+        sent_strips(window)
+
+    def left(turn, carried):
+        for leave in leaving((a + turn) % outer, turn):
+            leave.wait()
+        return carried
+
+    lax.fori_loop(0, outer, left, 0)
+
+
+def image_kernel(
+    raw_in,
+    light_in,
+    src_in,
+    rec_in,
+    image_out,
+    src_out,
+    rec_out,
+    raw,
+    light,
+    finals,
+    image,
+    inverse,
+    light_own,
+    raw_own,
+    final_own,
+    image_own,
+):
+    lags, depth = raw.shape[:2]
+    unit = raw.shape[2:]
+    get_light = pltpu.make_async_copy(light_in, light, light_own.at[0])
+    get_light.start()
+    gets = [
+        pltpu.make_async_copy(source, finals.at[index], final_own.at[0, index])
+        for index, source in enumerate((src_in, rec_in))
+    ]
+    puts = [
+        pltpu.make_async_copy(finals.at[index], landed, final_own.at[1, index])
+        for index, landed in enumerate((src_out, rec_out))
+    ]
+
+    def get_raw(index):
+        return pltpu.make_async_copy(raw_in.at[index], raw.at[index], raw_own.at[index])
+
+    def put_image(index):
+        return pltpu.make_async_copy(
+            image.at[index], image_out.at[index], image_own.at[index]
+        )
+
+    for get in gets:
+        get.start()
+    for index in range(lags):
+        get_raw(index).start()
+
+    pivots = []
+    pivot = 0.0
+    for _ in range(depth):
+        pivot = 1.0 / (1.0 + 2.0 * smoothing - smoothing * smoothing * pivot)
+        pivots.append(float(np.float32(pivot)))
+    settled = min(z for z in range(depth) if pivots[z] == pivots[-1])
+    settled = min(depth, -(-settled // 8) * 8)
+    get_light.wait()
+
+    def forward(z, pivot, carried):
+        value = light[z] * pivot + (smoothing * pivot) * carried
         inverse[z] = value
         return value
 
-    lax.fori_loop(0, depth, down, jnp.zeros(unit, jnp.float32), unroll=8)
-
-    def up(turn, carried):
-        z = depth - 1 - turn
-        value = inverse[z] + (smoothing * pivot_ref[z]) * carried
+    def backward(z, pivot, carried):
+        value = inverse[z] + (smoothing * pivot) * carried
         inverse[z] = 1.0 / (value + damping)
         return value
 
-    lax.fori_loop(0, depth, up, jnp.zeros(unit, jnp.float32), unroll=8)
-
-    lane = lax.broadcasted_iota(jnp.int32, unit, 1)
+    rest = (depth - settled) // 8
+    value = jnp.zeros(unit, jnp.float32)
+    for z in range(settled):
+        value = forward(z, pivots[z], value)
+
+    def down(turn, carried):
+        for step in range(8):
+            carried = forward(settled + turn * 8 + step, pivots[-1], carried)
+        return carried
+
+    lax.fori_loop(0, rest, down, value)
+    for get, put in zip(gets, puts):
+        get.wait()
+        put.start()
+
+    def up(turn, carried):
+        for step in range(8):
+            carried = backward(depth - 1 - turn * 8 - step, pivots[-1], carried)
+        return carried
+
+    value = lax.fori_loop(0, rest, up, jnp.zeros(unit, jnp.float32))
+    for z in reversed(range(settled)):
+        value = backward(z, pivots[z], value)
+
     some = 32
     for index in range(lags):
-        lag = lag_ref[index]
-        reach = jnp.abs(lag)
-        inside = (lane >= reach) & (lane < breadth - reach)
-        back = lax.rem(2 * breadth - 2 * lag, breadth)
-        forth = lax.rem(breadth + lag, breadth)
+        get_raw(index).wait()
 
         def layers(block, carried):
             z = pl.ds(block * some, some)
-            raw = strips[0, 0, z] * pltpu.roll(strips[0, 1, z], back, 2)
-            raw = raw + strips[1, 0, z] * pltpu.roll(strips[1, 1, z], back, 2)
-            raw = jnp.where(inside[None], pltpu.roll(raw, forth, 2), 0.0)
-            image[index, z] = (raw * inverse[z]).astype(jnp.bfloat16)
+            image[index, z] = (raw[index, z] * inverse[z]).astype(jnp.bfloat16)
             return carried
 
         lax.fori_loop(0, depth // some, layers, 0)
+        put_image(index).start()
+    for index in range(lags):
+        put_image(index).wait()
+    for put in puts:
+        put.wait()
 
 
 def local(
     count,
+    shots,
     source_now,
     source_before,
     receiver_now,
@@ -641,33 +853,45 @@
     height = wide // 2
     strip = wide // count
     tall = height * 8 * EPOCH // breadth
+    lags = lag_offsets.shape[0]
     me = lax.axis_index("gz")
-    weights_a, weights_b = lateral_weights(breadth)
-
-    any_space = pl.BlockSpec(memory_space=pl.ANY)
-    vmem = pl.BlockSpec(memory_space=pltpu.VMEM)
+
+    hbm = pl.BlockSpec(memory_space=pltpu.HBM)
     smem = pl.BlockSpec(memory_space=pltpu.SMEM)
     dma = pltpu.SemaphoreType.DMA
     flat = jax.ShapeDtypeStruct(source_now.shape, jnp.float32)
-    strips, source_final, receiver_final = pl.pallas_call(
-        functools.partial(wave_kernel, count, strip),
+    raw, light, source_final, receiver_final = pl.pallas_call(
+        functools.partial(wave_kernel, count, shots, strip),
         out_shape=(
-            jax.ShapeDtypeStruct((SNAPS, 2, depth, ROWS, breadth), jnp.float32),
+            jax.ShapeDtypeStruct((lags, depth, ROWS, breadth), jnp.float32),
+            jax.ShapeDtypeStruct((depth, ROWS, breadth), jnp.float32),
             flat,
             flat,
         ),
-        in_specs=[smem] * 2 + [any_space] * 5 + [vmem] * 4,
-        out_specs=(any_space, any_space, any_space),
+        in_specs=[smem] + [hbm] * 9,
+        out_specs=(hbm, hbm, hbm, hbm),
         scratch_shapes=[
+            pltpu.SMEM(snap_phase.shape, jnp.int32),
+            pltpu.SMEM(face_steps.shape, jnp.int32),
+            pltpu.VMEM(saved_faces.shape, jnp.float32),
+            pltpu.VMEM(traces.shape, traces.dtype),
+            pltpu.VMEM((2 * breadth, breadth), jnp.bfloat16),
+            pltpu.VMEM((breadth, breadth), jnp.bfloat16),
             pltpu.VMEM((2, layers + 2 * HALO, height + 2 * ROWS, breadth), jnp.float32),
             pltpu.VMEM((layers, height, breadth), jnp.float32),
             pltpu.VMEM((EPOCHS, 2, thin, tall, breadth), jnp.float32),
             pltpu.VMEM((EPOCHS, layers, tall, breadth), jnp.float32),
             pltpu.VMEM((2, 2, HALO, height, breadth), jnp.float32),
             pltpu.VMEM((SNAPS, layers, height, breadth), jnp.float32),
+            pltpu.VMEM((SNAPS, 2, depth, ROWS, breadth), jnp.float32),
+            pltpu.VMEM((lags, depth, ROWS, breadth), jnp.float32),
+            pltpu.VMEM((depth, ROWS, breadth), jnp.float32),
+            dma((4,)),
             dma((3, GROUP)),
             dma((3, GROUP)),
             dma((3,)),
+            dma((2,)),
+            dma((2,)),
             dma((EPOCHS, 2)),
             dma((EPOCHS, GROUP)),
             dma((2, 2, PIECES)),
@@ -680,12 +904,14 @@
             dma((GROUP,)),
             dma((2, 2)),
             dma((1,)),
+            dma((2, outer)),
         ],
         compiler_params=pltpu.CompilerParams(
-            has_side_effects=True, vmem_limit_bytes=40 * 1024 * 1024
+            has_side_effects=True, vmem_limit_bytes=VMEM_BYTES
         ),
         name="waves",
     )(
+        lag_offsets,
         snap_phase,
         face_steps,
         source_now,
@@ -695,34 +921,37 @@
         speed_term,
         saved_faces,
         traces,
-        weights_a,
-        weights_b,
     )
 
     if strip < ROWS:
-        strips = lax.dynamic_slice_in_dim(strips, (me * strip) % ROWS, strip, 3)
-    pivots = []
-    pivot = 0.0
-    for _ in range(depth):
-        pivot = 1.0 / (1.0 + 2.0 * smoothing - smoothing * smoothing * pivot)
-        pivots.append(pivot)
-    image = pl.pallas_call(
+        place = (me * strip) % ROWS
+        raw = lax.dynamic_slice_in_dim(raw, place, strip, 2)
+        light = lax.dynamic_slice_in_dim(light, place, strip, 1)
+    image_shape = (lags, depth, strip, breadth)
+    return pl.pallas_call(
         image_kernel,
-        out_shape=jax.ShapeDtypeStruct(
-            (lag_offsets.shape[0], depth, strip, breadth), jnp.bfloat16
-        ),
-        in_specs=[smem, smem, vmem],
-        out_specs=vmem,
-        scratch_shapes=[pltpu.VMEM((depth, strip, breadth), jnp.float32)],
-        compiler_params=pltpu.CompilerParams(vmem_limit_bytes=48 * 1024 * 1024),
+        out_shape=(jax.ShapeDtypeStruct(image_shape, jnp.bfloat16), flat, flat),
+        in_specs=[hbm] * 4,
+        out_specs=(hbm, hbm, hbm),
+        scratch_shapes=[
+            pltpu.VMEM(raw.shape, jnp.float32),
+            pltpu.VMEM(light.shape, jnp.float32),
+            pltpu.VMEM((2,) + source_now.shape, jnp.float32),
+            pltpu.VMEM(image_shape, jnp.bfloat16),
+            pltpu.VMEM(light.shape, jnp.float32),
+            dma((1,)),
+            dma((lags,)),
+            dma((2, 2)),
+            dma((lags,)),
+        ],
+        compiler_params=pltpu.CompilerParams(vmem_limit_bytes=VMEM_BYTES),
         name="images",
-    )(lag_offsets, jnp.asarray(np.array(pivots, np.float32)), strips)
-    return image, source_final, receiver_final
+    )(raw, light, source_final, receiver_final)
 
 
 def solution(mesh):
     return jax.shard_map(
-        functools.partial(local, mesh.shape["gz"]),
+        functools.partial(local, mesh.shape["gz"], mesh.shape["shot"]),
         mesh=mesh,
         in_specs=(
             P(("shot", "gz"), None, None),

time: 162 us -> 142 us (0.88)
  the two profiles are of different devices: /device:TPU:1 before, /device:TPU:15 now
where the time goes in v2:
time: 142 us; the launch traced here: 140 us
  Pallas kernels  139 us (98%)
    pallas_call x1, Pallas kernels, local(): pl.pallas_call(functools.partial(wave_kernel, count, shots, strip), out_s...  134 us
    pallas_call x1, Pallas kernels, local(): pl.pallas_call(image_kernel, out_shape=(jax.ShapeDtypeStruct(image_shape,...  5.09 us

profile of v2, /device:TPU:15, one launch (start us, length us, event | category | flops | bytes accessed | tf_op | source)
XLA Modules:
  0.0 139.6 jit_solution(6162773790152663297)
XLA Ops:
  0.6 133.9 %waves.1 = (f32[8,128,8,128]{3,2,1,0:T(8,128)}, f32[128,8,128]{2,1,0:T(8,128)}, f32[8,128,128]{2,1,0:T(8,128)}, f32[8,128,128]{2,1,0:T(8,128)}) custom-call(s32[8]{0:T(128)} %lag_ref.1, s32[2]{0:T(128)} %phase_hbm.1, s32[12]{0:T(128)} %order_hbm.1, f32[8,128,128]{2,1,0:T(8,128)} %src_now.1, f32[8,128,128]{2,1,0:T(8,128)} %src_old.1, f32[8,128,128]{2,1,0:T(8,128)} %rec_now.1, ...), custom_call_target="tpu_custom_call" | custom-call | tf_op jit(solution)/shard_map/waves/pallas_call | solution.py:863
  134.6 5.1 %images.1 = (bf16[8,128,8,128]{3,2,1,0:T(8,128)(2,1)}, f32[8,128,128]{2,1,0:T(8,128)}, f32[8,128,128]{2,1,0:T(8,128)}) custom-call(f32[8,128,8,128]{3,2,1,0:T(8,128)} %get-tuple-element.7.raw_in, f32[128,8,128]{2,1,0:T(8,128)} %get-tuple-element.8.light_in, f32[8,128,128]{2,1,0:T(8,128)} %get-tuple-element.9.src_in, f32[8,128,128]{2,1,0:T(8,128)} %get-tuple-element.10.rec_in), custom_call_target="tpu_custom_call" | custom-call | tf_op jit(solution)/shard_map/images/pallas_call | solution.py:931

commit v3 on v2

--- a/solution.py
+++ b/solution.py
@@ -230,6 +230,7 @@
     across = 8 * EPOCH
     groups = breadth // across
     tall = height // groups
+    tiles_a_part = tall // ROWS
     for z in range(thin):
         parts = [
             pltpu.roll(faces[order_ref[step], :, z, :], 4, 0) for step in range(STEPS)
@@ -387,10 +388,18 @@
     outside = ((lane < 4) | (lane >= breadth - 4)) & (kind == 0)
     lit = jnp.logical_and(a == 0, kind == 1)
 
-    def partial(step, now, later, base, top):
-        planes = pl.ds(HALO + base, CHUNK)
-        center = field[now, planes, inner, :]
-        flat = center.reshape(CHUNK * height, breadth)
+    tiles = height // ROWS
+
+    def partial(step, now, later, base, deep, first, many, top=False):
+        planes = pl.ds(HALO + base, deep)
+        start = first * ROWS
+        if not isinstance(first, int):
+            start = pl.multiple_of(start, ROWS)
+        tall = many * ROWS
+        rows = pl.ds(ROWS + start, tall)
+        window = field[now, planes, pl.ds(start, tall + 2 * ROWS), :]
+        center = window[:, ROWS : ROWS + tall]
+        flat = center.reshape(deep * tall, breadth)
         high = flat.astype(jnp.bfloat16)
         low = (flat - high.astype(jnp.float32)).astype(jnp.bfloat16)
         lateral = jnp.dot(
@@ -398,34 +407,33 @@
             weights_a[...],
             preferred_element_type=jnp.float32,
         ) + jnp.dot(high, weights_b[...], preferred_element_type=jnp.float32)
-        summed = lateral.reshape(CHUNK, height, breadth)
+        summed = lateral.reshape(deep, tall, breadth)
         for offset in range(1, 5):
             summed = summed + stencil_weights[offset] * (
                 (
-                    field[now, pl.ds(HALO + base + offset, CHUNK), inner, :]
-                    + field[now, pl.ds(HALO + base - offset, CHUNK), inner, :]
+                    field[now, pl.ds(HALO + base + offset, deep), rows, :]
+                    + field[now, pl.ds(HALO + base - offset, deep), rows, :]
                 )
                 + (
-                    field[now, planes, pl.ds(ROWS + offset, height), :]
-                    + field[now, planes, pl.ds(ROWS - offset, height), :]
+                    window[:, ROWS + offset : ROWS + offset + tall]
+                    + window[:, ROWS - offset : ROWS - offset + tall]
                 )
             )
-        previous = field[later, planes, inner, :]
-        updated = 2.0 * center - previous + factor[pl.ds(base, CHUNK)] * summed
-        edge = edges[step // EPOCH, pl.ds(base, CHUNK)].reshape(CHUNK * tall, breadth)
-        placed = jnp.concatenate(
-            [
-                pltpu.roll(
-                    edge,
-                    lax.rem(
-                        3 * breadth - 4 - across * part - 8 * (step % EPOCH), breadth
-                    ),
-                    1,
-                ).reshape(CHUNK, tall, breadth)
-                for part in range(groups)
-            ],
-            axis=1,
-        )
+        previous = field[later, planes, rows, :]
+        speeds = factor[pl.ds(base, deep), pl.ds(start, tall)]
+        updated = 2.0 * center - previous + speeds * summed
+        placed = []
+        for tile in range(many):
+            place = first + tile
+            inside = place % tiles_a_part * ROWS
+            if not isinstance(place, int):
+                inside = pl.multiple_of(inside, ROWS)
+            edge = edges[step // EPOCH, pl.ds(base, deep), pl.ds(inside, ROWS)]
+            turn = 3 * breadth - 4 - across * (place // tiles_a_part)
+            turn = lax.rem(turn - 8 * (step % EPOCH), breadth)
+            edge = pltpu.roll(edge.reshape(deep * ROWS, breadth), turn, 1)
+            placed.append(edge.reshape(deep, ROWS, breadth))
+        placed = placed[0] if many == 1 else jnp.concatenate(placed, axis=1)
         updated = jnp.where(outside, placed, updated)
         if top:
             trace = traces[step, pl.ds(pl.multiple_of(c * height, height), height)]
@@ -460,8 +468,6 @@
             field[later, planes, wide] = value
             keep(window, take, base, rows, value)
 
-    whole = pl.ds(0, height)
-
     def whole_step(window, local):
         step = window * SNAP_EVERY + local
         now = lax.rem(step, 2)
@@ -475,23 +481,29 @@
 
         wait_row(now)
         for base, top in ((0, True), (layers - HALO, False)):
-            field[later, pl.ds(HALO + base, CHUNK), inner] = partial(
-                step, now, later, base, top
+            field[later, pl.ds(HALO + base, HALO), inner] = partial(
+                step, now, later, base, HALO, 0, tiles, top
             )
         for piece in range(PIECES):
             wait_z(piece, now)
             complete(window, take, now, later, piece)
             send_z(piece, later, more)
 
+        def interior(base, deep, first, many):
+            start = pl.multiple_of(first * ROWS, ROWS)
+            value = partial(step, now, later, base, deep, first, many)
+            rows = pl.ds(ROWS + start, many * ROWS)
+            field[later, pl.ds(HALO + base, deep), rows] = value
+            keep(window, take, base, pl.ds(start, many * ROWS), value)
+
+        interior(HALO, layers - 2 * HALO, (1 - c) * (tiles - 1), 1)
+        send_row(later, more)
+
         def middle(chunk, carried):
-            base = chunk * CHUNK
-            value = partial(step, now, later, base, False)
-            field[later, pl.ds(HALO + base, CHUNK), inner] = value
-            keep(window, take, base, whole, value)
+            interior(chunk * CHUNK, CHUNK, c, tiles - 1)
             return carried
 
         lax.fori_loop(1, layers // CHUNK - 1, middle, 0)
-        send_row(later, more)
         sent_z(now)
         sent_row(now)
 

time: 142 us -> 137 us (0.965); the launches traced: 140 us -> 137 us
  Pallas kernels: 139 us -> 136 us
    pallas_call x1, Pallas kernels: 134 us -> 131 us  [local(): pl.pallas_call(functools.partial(wave_kernel, count, shots, strip), out_s...]
where the time goes in v3:
time: 137 us
  Pallas kernels  136 us (99%)
    pallas_call x1, Pallas kernels, local(): pl.pallas_call(functools.partial(wave_kernel, count, shots, strip), out_s...  131 us
    pallas_call x1, Pallas kernels, local(): pl.pallas_call(image_kernel, out_shape=(jax.ShapeDtypeStruct(image_shape,...  5.09 us

profile of v3, /device:TPU:15, one launch (start us, length us, event | category | flops | bytes accessed | tf_op | source)
XLA Modules:
  0.0 136.7 jit_solution(5095889640118063114)
XLA Ops:
  0.6 130.9 %waves.1 = (f32[8,128,8,128]{3,2,1,0:T(8,128)}, f32[128,8,128]{2,1,0:T(8,128)}, f32[8,128,128]{2,1,0:T(8,128)}, f32[8,128,128]{2,1,0:T(8,128)}) custom-call(s32[8]{0:T(128)} %lag_ref.1, s32[2]{0:T(128)} %phase_hbm.1, s32[12]{0:T(128)} %order_hbm.1, f32[8,128,128]{2,1,0:T(8,128)} %src_now.1, f32[8,128,128]{2,1,0:T(8,128)} %src_old.1, f32[8,128,128]{2,1,0:T(8,128)} %rec_now.1, ...), custom_call_target="tpu_custom_call" | custom-call | tf_op jit(solution)/shard_map/waves/pallas_call | solution.py:875
  131.6 5.1 %images.1 = (bf16[8,128,8,128]{3,2,1,0:T(8,128)(2,1)}, f32[8,128,128]{2,1,0:T(8,128)}, f32[8,128,128]{2,1,0:T(8,128)}) custom-call(f32[8,128,8,128]{3,2,1,0:T(8,128)} %get-tuple-element.7.raw_in, f32[128,8,128]{2,1,0:T(8,128)} %get-tuple-element.8.light_in, f32[8,128,128]{2,1,0:T(8,128)} %get-tuple-element.9.src_in, f32[8,128,128]{2,1,0:T(8,128)} %get-tuple-element.10.rec_in), custom_call_target="tpu_custom_call" | custom-call | tf_op jit(solution)/shard_map/images/pallas_call | solution.py:943

commit v4 on v3

--- a/solution.py
+++ b/solution.py
@@ -37,6 +37,10 @@
     high = band.astype(jnp.bfloat16)
     low = (band - high.astype(jnp.float32)).astype(jnp.bfloat16)
     return high, low
+
+
+def close_barrier(outer):
+    return outer <= SNAP_EVERY
 
 
 def wave_kernel(
@@ -107,6 +111,41 @@
     old_of = (src_old, rec_old)
     outs = (src_out, rec_out)
 
+    paired = shots % 2 == 0
+    shot = lax.axis_index("shot")
+    parity = shot % 2
+    other_shot = {"shot": shot + 1 - 2 * parity, "gz": me}
+
+    if close_barrier(outer):
+        barrier = pltpu.get_barrier_semaphore()
+
+        def greet(device):
+            pl.semaphore_signal(barrier, inc=1, device_id=device, device_id_type=MESH)
+
+        for shift in range(1, GROUP):
+            greet({"gz": a * GROUP + (b + shift) % GROUP})
+        if paired:
+            greet(other_shot)
+
+        @pl.when(a > 0)
+        def _():
+            greet({"gz": me - GROUP})
+
+        @pl.when(a < outer - 1)
+        def _():
+            greet({"gz": me + GROUP})
+
+        beside = (a > 0, a < outer - 1)
+        for count_beside, met in (
+            (2, jnp.logical_and(*beside)),
+            (1, beside[0] != beside[1]),
+            (0, jnp.logical_not(jnp.logical_or(*beside))),
+        ):
+
+            @pl.when(met)
+            def _():
+                pl.semaphore_wait(barrier, GROUP - 1 + paired + count_beside)
+
     def load_refs(index, target, sender):
         rows = pl.ds(target % 2 * height, height)
         planes = pl.ds(HALO + sender * thin, thin)
@@ -133,10 +172,6 @@
         source, landed = load_refs(index, target, target)
         return pltpu.make_async_copy(source, landed, load_own.at[index])
 
-    paired = shots % 2 == 0
-    shot = lax.axis_index("shot")
-    parity = shot % 2
-
     def direct(index, target):
         if index > 0 or not paired:
             return b != target
@@ -150,7 +185,7 @@
             dst_ref=view,
             send_sem=relay_send.at[sender % 2],
             recv_sem=relay_recv.at[sender % 2],
-            device_id={"shot": shot + 1 - 2 * parity, "gz": me},
+            device_id=other_shot,
             device_id_type=MESH,
         )
 
@@ -919,7 +954,9 @@
             dma((2, outer)),
         ],
         compiler_params=pltpu.CompilerParams(
-            has_side_effects=True, vmem_limit_bytes=VMEM_BYTES
+            has_side_effects=True,
+            vmem_limit_bytes=VMEM_BYTES,
+            collective_id=0 if close_barrier(outer) else None,
         ),
         name="waves",
     )(

time: 137 us -> 134 us (0.978)
  Pallas kernels: 136 us -> 133 us
    pallas_call x1, Pallas kernels: 131 us -> 128 us  [local(): pl.pallas_call(functools.partial(wave_kernel, count, shots, strip), out_s...]
where the time goes in v4:
time: 134 us; the launch traced here: 133 us
  Pallas kernels  133 us (99%)
    pallas_call x1, Pallas kernels, local(): pl.pallas_call(functools.partial(wave_kernel, count, shots, strip), out_s...  128 us
    pallas_call x1, Pallas kernels, local(): pl.pallas_call(image_kernel, out_shape=(jax.ShapeDtypeStruct(image_shape,...  5.09 us

profile of v4, /device:TPU:15, one launch (start us, length us, event | category | flops | bytes accessed | tf_op | source)
XLA Modules:
  0.0 133.4 jit_solution(14430536883243026090)
XLA Ops:
  0.6 127.6 %waves.1 = (f32[8,128,8,128]{3,2,1,0:T(8,128)}, f32[128,8,128]{2,1,0:T(8,128)}, f32[8,128,128]{2,1,0:T(8,128)}, f32[8,128,128]{2,1,0:T(8,128)}) custom-call(s32[8]{0:T(128)} %lag_ref.1, s32[2]{0:T(128)} %phase_hbm.1, s32[12]{0:T(128)} %order_hbm.1, f32[8,128,128]{2,1,0:T(8,128)} %src_now.1, f32[8,128,128]{2,1,0:T(8,128)} %src_old.1, f32[8,128,128]{2,1,0:T(8,128)} %rec_now.1, ...), custom_call_target="tpu_custom_call" | custom-call | tf_op jit(solution)/shard_map/waves/pallas_call | solution.py:910
  128.3 5.1 %images.1 = (bf16[8,128,8,128]{3,2,1,0:T(8,128)(2,1)}, f32[8,128,128]{2,1,0:T(8,128)}, f32[8,128,128]{2,1,0:T(8,128)}) custom-call(f32[8,128,8,128]{3,2,1,0:T(8,128)} %get-tuple-element.7.raw_in, f32[128,8,128]{2,1,0:T(8,128)} %get-tuple-element.8.light_in, f32[8,128,128]{2,1,0:T(8,128)} %get-tuple-element.9.src_in, f32[8,128,128]{2,1,0:T(8,128)} %get-tuple-element.10.rec_in), custom_call_target="tpu_custom_call" | custom-call | tf_op jit(solution)/shard_map/images/pallas_call | solution.py:980

commit v5 on v4

--- a/solution.py
+++ b/solution.py
@@ -15,7 +15,7 @@
 ROWS = 8
 CHUNK = 4
 GROUP = 4
-PIECES = 4
+PIECES = 8
 EPOCH = 4
 VMEM_BYTES = 60 * 1024 * 1024
 EPOCHS = STEPS // EPOCH

time: 134 us -> 135 us (level)
  no operation moved by 1% of the time
where the time goes in v5:
time: 135 us; the launch traced here: 134 us
  Pallas kernels  134 us (99%)
    pallas_call x1, Pallas kernels, local(): pl.pallas_call(functools.partial(wave_kernel, count, shots, strip), out_s...  129 us
    pallas_call x1, Pallas kernels, local(): pl.pallas_call(image_kernel, out_shape=(jax.ShapeDtypeStruct(image_shape,...  5.09 us

profile of v5, /device:TPU:15, one launch (start us, length us, event | category | flops | bytes accessed | tf_op | source)
XLA Modules:
  0.0 134.5 jit_solution(7471929554374449234)
XLA Ops:
  0.6 128.8 %waves.1 = (f32[8,128,8,128]{3,2,1,0:T(8,128)}, f32[128,8,128]{2,1,0:T(8,128)}, f32[8,128,128]{2,1,0:T(8,128)}, f32[8,128,128]{2,1,0:T(8,128)}) custom-call(s32[8]{0:T(128)} %lag_ref.1, s32[2]{0:T(128)} %phase_hbm.1, s32[12]{0:T(128)} %order_hbm.1, f32[8,128,128]{2,1,0:T(8,128)} %src_now.1, f32[8,128,128]{2,1,0:T(8,128)} %src_old.1, f32[8,128,128]{2,1,0:T(8,128)} %rec_now.1, ...), custom_call_target="tpu_custom_call" | custom-call | tf_op jit(solution)/shard_map/waves/pallas_call | solution.py:910
  129.4 5.1 %images.1 = (bf16[8,128,8,128]{3,2,1,0:T(8,128)(2,1)}, f32[8,128,128]{2,1,0:T(8,128)}, f32[8,128,128]{2,1,0:T(8,128)}) custom-call(f32[8,128,8,128]{3,2,1,0:T(8,128)} %get-tuple-element.7.raw_in, f32[128,8,128]{2,1,0:T(8,128)} %get-tuple-element.8.light_in, f32[8,128,128]{2,1,0:T(8,128)} %get-tuple-element.9.src_in, f32[8,128,128]{2,1,0:T(8,128)} %get-tuple-element.10.rec_in), custom_call_target="tpu_custom_call" | custom-call | tf_op jit(solution)/shard_map/images/pallas_call | solution.py:980
